TPU v7x, 32 devices: a whole 2x2x4 slice. The times are simulated.
32 devices in a mesh: member: 2 (over y), slab: 4 (over z), chan: 2 (over x), mode: 2 (over core).
Axes of the slice: x: 2, y: 2, z: 4, core: 2. Of those that a mesh axis runs over, the one named last changes fastest.
Arguments:
- source_field: float32 [128, 1024, 1024], P(('member', 'chan'), 'slab', 'mode'), parts along dimension 0, may hold values from -6 to 6
- cotangent: float32 [128, 1024, 1024], P(('member', 'chan'), 'slab', 'mode'), parts along dimension 0, may hold values from -6 to 6
- spectral_weight: float32 [128, 64, 32, 2, 64], P(('member', 'chan'), None, 'mode', None, 'slab'), parts along dimension 0, may hold values from -12 to 12
- skip_gain: float32 [128], P(('member', 'chan')), parts along dimension 0, may hold values from 0.5 to 2
- channel_bias: float32 [128], P(('member', 'chan')), parts along dimension 0, may hold values from -0.5 to 0.5
- mode_limit: int32 [128, 2], P('member'), parts along dimension 0, may hold values from 16 to 32
- width_limit: int32 [128], P('member'), parts along dimension 0, may hold values from 32 to 64
Outputs:
- output: float32 [128, 1024, 1024], P(('member', 'chan'), 'slab', 'mode'), parts along dimension 0
- field_grad: float32 [128, 1024, 1024], P(('member', 'chan'), 'slab', 'mode'), parts along dimension 0
- spectral_grad: float32 [128, 64, 32, 2, 64], P(('member', 'chan'), None, 'mode', None, 'slab'), parts along dimension 0
- gate_grad: float32 [128], P(('member', 'chan')), parts along dimension 0
- bias_grad: float32 [128], P(('member', 'chan')), parts along dimension 0
There are 2 independent parts, one for each index of `member`. A program takes and returns all parts, laid end to end along the dimension named above; each array names one. Nothing has to cross between parts.
Inputs may be any that keep to these rules, and one draw needn't show every extreme that they name: `mode_limit`: never more than 32. `width_limit`: never more than 64.
All inputs are finite; a program needn't handle non-finite values.
Results may differ from a plain program's by a relative error of at most 0.00018.
Values sent between devices are 32-bit elements; how exact they have to be, the bound alone decides.
No kernel may reach another device: no remote copies, remote signals or barrier semaphores. Data moves between devices by JAX's collectives and lax.ppermute only.
A program may use at most 192 MiB of HBM per device.

v0:
```python
import math
import jax
import jax.numpy as jnp
from jax import lax
from jax.sharding import PartitionSpec as P

precise = lax.Precision.HIGHEST


def column_table(extent, freq_count, first_cell, cell_count):
    cell_index = first_cell + jnp.arange(cell_count, dtype=jnp.int32)
    wave_index = jnp.arange(freq_count, dtype=jnp.int32)
    products = (cell_index[:, None] * wave_index[None, :] % extent).astype(jnp.float32)
    angles = products * (2.0 * math.pi / extent)
    return jnp.stack([jnp.cos(angles), -jnp.sin(angles)], axis=-1).reshape(
        cell_count, 2 * freq_count
    )


def row_tables(extent, freq_count, first_cell, cell_count):
    cell_index = first_cell + jnp.arange(cell_count, dtype=jnp.int32)
    column = jnp.arange(2 * freq_count, dtype=jnp.int32)
    wave_index = column + jnp.where(column >= freq_count, extent - 2 * freq_count, 0)
    products = (cell_index[:, None] * wave_index[None, :] % extent).astype(jnp.float32)
    angles = products * (2.0 * math.pi / extent)
    return (jnp.cos(angles), jnp.sin(angles))


def row_forward(lined, row_cos, row_sin):
    line_real = lined[:, 0]
    line_imag = lined[:, 1]
    out_real = jnp.dot(line_real, row_cos, precision=precise) + jnp.dot(
        line_imag, row_sin, precision=precise
    )
    out_imag = jnp.dot(line_imag, row_cos, precision=precise) - jnp.dot(
        line_real, row_sin, precision=precise
    )
    return jnp.stack([out_real, out_imag], axis=1)


def row_inverse(modes_in, row_cos, row_sin):
    mode_real = modes_in[:, 0]
    mode_imag = modes_in[:, 1]
    back_real = jnp.dot(mode_real, row_cos.T, precision=precise) - jnp.dot(
        mode_imag, row_sin.T, precision=precise
    )
    back_imag = jnp.dot(mode_real, row_sin.T, precision=precise) + jnp.dot(
        mode_imag, row_cos.T, precision=precise
    )
    return jnp.stack([back_real, back_imag], axis=1)


def contract(spectra, weight):
    spec_real = spectra[:, :, 0]
    spec_imag = spectra[:, :, 1]
    weight_real = weight[:, :, :, 0]
    weight_imag = weight[:, :, :, 1]
    out_real = jnp.einsum("iyx,ioyx->oyx", spec_real, weight_real, precision=precise) - jnp.einsum(
        "iyx,ioyx->oyx", spec_imag, weight_imag, precision=precise
    )
    out_imag = jnp.einsum("iyx,ioyx->oyx", spec_real, weight_imag, precision=precise) + jnp.einsum(
        "iyx,ioyx->oyx", spec_imag, weight_real, precision=precise
    )
    return jnp.stack([out_real, out_imag], axis=2)


def contract_back(grads, weight):
    grad_real = grads[:, :, 0]
    grad_imag = grads[:, :, 1]
    weight_real = weight[:, :, :, 0]
    weight_imag = weight[:, :, :, 1]
    back_real = jnp.einsum("oyx,ioyx->iyx", grad_real, weight_real, precision=precise) + jnp.einsum(
        "oyx,ioyx->iyx", grad_imag, weight_imag, precision=precise
    )
    back_imag = jnp.einsum("oyx,ioyx->iyx", grad_imag, weight_real, precision=precise) - jnp.einsum(
        "oyx,ioyx->iyx", grad_real, weight_imag, precision=precise
    )
    return jnp.stack([back_real, back_imag], axis=2)


def outer_grad(spectra, grads):
    spec_real = spectra[:, :, 0]
    spec_imag = spectra[:, :, 1]
    grad_real = grads[:, :, 0]
    grad_imag = grads[:, :, 1]
    real_side = jnp.einsum("iyx,oyx->ioyx", spec_real, grad_real) + jnp.einsum(
        "iyx,oyx->ioyx", spec_imag, grad_imag
    )
    imag_side = jnp.einsum("iyx,oyx->ioyx", spec_real, grad_imag) - jnp.einsum(
        "iyx,oyx->ioyx", spec_imag, grad_real
    )
    return jnp.stack([real_side, imag_side], axis=3)


def mode_weights(limit_rows, col_freq, row_freq, kx_count, cells_total):
    keep_cols = col_freq[None, :] < limit_rows[:, 0:1]
    keep_rows = (row_freq[None, :] < limit_rows[:, 1:2]) | (
        (kx_count - row_freq)[None, :] < limit_rows[:, 1:2]
    )
    scales = jnp.where(col_freq == 0, 1.0, 2.0).astype(jnp.float32) / cells_total
    joined = keep_cols[:, :, None] & keep_rows[:, None, :]
    return (joined.astype(jnp.float32) * scales[None, :, None])[:, :, None, :]


def read_mask(in_index, width_limit):
    return (in_index[:, None] < width_limit[None, :]).astype(jnp.float32)[:, :, None, None, None]


def local(
    source_field, cotangent, spectral_weight, skip_gain, channel_bias, mode_limit, width_limit
):
    channels, row_count, col_count = source_field.shape
    slab_count = lax.axis_size("slab")
    mode_count = lax.axis_size("mode")
    slab_index = lax.axis_index("slab")
    mode_index = lax.axis_index("mode")
    chan_index = lax.axis_index("chan")
    local_freq = spectral_weight.shape[2]
    local_kx = spectral_weight.shape[4]
    freq_count = local_freq * mode_count
    kx_count = local_kx * slab_count
    all_rows = row_count * slab_count
    all_cols = col_count * mode_count
    column_tab = column_table(all_cols, freq_count, mode_index * col_count, col_count)
    row_cos, row_sin = row_tables(all_rows, freq_count, slab_index * row_count, row_count)

    def spectrum(values):
        partial_cols = jnp.einsum("chw,wk->ckh", values, column_tab, precision=precise)
        summed_cols = lax.psum_scatter(partial_cols, "mode", scatter_dimension=1, tiled=True)
        paired = summed_cols.reshape(values.shape[0] * local_freq, 2, row_count)
        spectra = lax.psum_scatter(
            row_forward(paired, row_cos, row_sin), "slab", scatter_dimension=2, tiled=True
        )
        return spectra.reshape(values.shape[0], local_freq, 2, local_kx)

    def synthesis(modes_in):
        whole_modes = lax.all_gather(modes_in, "slab", axis=3, tiled=True)
        rebuilt = row_inverse(
            whole_modes.reshape(channels * local_freq, 2, kx_count), row_cos, row_sin
        )
        rebuilt = rebuilt.reshape(channels, 2 * local_freq, row_count)
        gathered = lax.all_gather(rebuilt, "mode", axis=1, tiled=True)
        return jnp.einsum("ckh,wk->chw", gathered, column_tab, precision=precise)

    in_index = chan_index * channels + jnp.arange(channels, dtype=jnp.int32)
    col_freq = mode_index * local_freq + jnp.arange(local_freq, dtype=jnp.int32)
    row_freq = slab_index * local_kx + jnp.arange(local_kx, dtype=jnp.int32)
    limit_rows = lax.dynamic_slice_in_dim(mode_limit, chan_index * channels, channels, 0)
    weights = mode_weights(limit_rows, col_freq, row_freq, kx_count, all_rows * all_cols)
    reads = read_mask(in_index, width_limit)
    masked_weight = spectral_weight * reads
    spectra = spectrum(source_field)
    out_modes = (
        lax.psum_scatter(contract(spectra, masked_weight), "chan", scatter_dimension=0, tiled=True)
        * weights
    )
    branch = synthesis(out_modes)
    skip_scale = skip_gain[:, None, None]
    summed = branch + skip_scale * source_field + channel_bias[:, None, None]
    output, gelu_back = jax.vjp(jax.nn.gelu, summed)
    grad_sum = gelu_back(cotangent)[0]
    grad_modes = spectrum(grad_sum) * weights
    all_grads = lax.all_gather(grad_modes, "chan", axis=0, tiled=True)
    spectral_grad = outer_grad(spectra, all_grads) * reads
    field_grad = synthesis(contract_back(all_grads, masked_weight)) + skip_scale * grad_sum
    gate_grad, bias_grad = lax.psum(
        (jnp.sum(grad_sum * source_field, axis=(1, 2)), jnp.sum(grad_sum, axis=(1, 2))),
        ("slab", "mode"),
    )
    return (output, field_grad, spectral_grad, gate_grad, bias_grad)


def solution(mesh):
    in_specs = (
        P(("member", "chan"), "slab", "mode"),
        P(("member", "chan"), "slab", "mode"),
        P(("member", "chan"), None, "mode", None, "slab"),
        P(("member", "chan")),
        P(("member", "chan")),
        P("member", None),
        P("member"),
    )
    out_specs = (
        P(("member", "chan"), "slab", "mode"),
        P(("member", "chan"), "slab", "mode"),
        P(("member", "chan"), None, "mode", None, "slab"),
        P(("member", "chan")),
        P(("member", "chan")),
    )
    return jax.shard_map(local, mesh=mesh, in_specs=in_specs, out_specs=out_specs, check_vma=False)
```

profile of v0, /device:TPU:0, one launch (start us, length us, event | category | flops | bytes accessed | tf_op | source)
XLA Modules:
  0.0 418.1 jit_solution(5773580187036393755)
XLA Ops:
  7.2 0.3 fusion.83
  7.8 20.7 %convolution_bitcast_fusion.1 = f32[32,64,256]{2,1,0:T(8,128)} fusion(f32[512,64,1]{0,1,2:T(8,128)S(1)} %reshape.294, f32[32,256,512]{2,1,0:T(8,128)} %param.7), kind=kOutput, calls=%fused_computation.35 | convolution fusion | flops 3221225472 | bytes 19005440 | tf_op jit(solution)/shard_map/chw,wk->ckh/dot_general | solution.py:128
  28.5 0.3 reduce-scatter.8.cloned.1.call-start
  29.2 0.6 copy-done.5
  29.8 8.5 %broadcast_multiply_fusion = f32[32,64,16,2,16]{1,4,3,2,0:T(8,128)} fusion(f32[32,64,16,2,16]{1,4,3,2,0:T(8,128)} %param.9, f32[32,64]{1,0:T(8,128)S(1)} %compare_convert_fusion), kind=kLoop, calls=%fused_computation.17 | loop fusion | flops 1048576 | bytes 8396800 | tf_op jit(solution)/shard_map/mul | solution.py:151
  38.3 2.7 reduce-scatter.6.cloned.1.call-done
  41.0 1.8 reshape.286
  42.9 0.8 fusion.153
  43.7 1.2 fusion.40
  44.9 1.2 fusion.36
  46.1 1.2 fusion.29
  47.3 1.2 fusion.28
  48.5 0.7 pad_maximum_fusion.2
  49.2 0.3 reduce-scatter.10.cloned.1.call-start
  49.5 7.8 %slice_bitcast_fusion.1 = (f32[32,64,16,16]{1,3,2,0:T(8,128)}, f32[32,64,16,16]{1,3,2,0:T(8,128)}) fusion(f32[32,64,16,2,16]{1,4,3,2,0:T(8,128)} %broadcast_multiply_fusion), kind=kLoop, calls=%fused_computation.14 | loop fusion | bytes 8388608 | tf_op jit(solution)/shard_map/squeeze | solution.py:56
  57.3 13.4 %reduce-scatter.8.cloned.1.call-done = f32[512,2,16]{0,2,1:T(8,128)} async-done(((f32[512,2,64]{0,2,1:T(8,128)}), f32[512,2,16]{0,2,1:T(8,128)}) %reduce-scatter.8.cloned.1.call-update) | async-done | bytes 65552 | tf_op jit(solution)/shard_map/reduce_scatter | solution.py:131
  70.7 1.0 reshape.287
  72.1 8.3 %fusion.18 = f32[16,16,1,64]{3,2,1,0:T(1,128)S(1)} fusion(f32[32,16,16,1]{0,3,2,1:T(1,128)S(1)} %copy.60, f32[32,64,16,16]{1,3,2,0:T(8,128)} %get-tuple-element.11), kind=kOutput, calls=%fused_computation.30 | convolution fusion | flops 6291456 | bytes 2195456 | tf_op jit(solution)/shard_map/iyx,ioyx->oyx/dot_general | solution.py:61
  80.5 8.6 %fusion.12 = f32[16,16,1,64]{3,2,1,0:T(1,128)S(1)} fusion(f32[32,16,16,1]{0,3,2,1:T(1,128)S(1)} %copy.60, f32[32,64,16,16]{1,3,2,0:T(8,128)} %get-tuple-element.12), kind=kOutput, calls=%fused_computation.24 | convolution fusion | flops 6291456 | bytes 2195456 | tf_op jit(solution)/shard_map/iyx,ioyx->oyx/dot_general | solution.py:58
  89.1 6.0 %fusion.20 = f32[16,16,1,64]{3,2,1,0:T(1,128)S(1)} fusion(f32[32,16,16,1]{0,3,2,1:T(1,128)S(1)} %copy.57, f32[32,64,16,16]{1,3,2,0:T(8,128)S(1)} %copy-done.3), kind=kOutput, calls=%fused_computation.32 | convolution fusion | flops 6291456 | bytes 2195456 | tf_op jit(solution)/shard_map/iyx,ioyx->oyx/dot_general | solution.py:58
  95.2 6.2 %fusion.10 = f32[16,16,1,64]{3,2,1,0:T(1,128)S(1)} fusion(f32[32,16,16,1]{0,3,2,1:T(1,128)S(1)} %copy.57, f32[32,64,16,16]{1,3,2,0:T(8,128)S(1)} %copy-done.2), kind=kOutput, calls=%fused_computation.22 | convolution fusion | flops 6291456 | bytes 2195456 | tf_op jit(solution)/shard_map/iyx,ioyx->oyx/dot_general | solution.py:61
  101.5 1.3 copy.46
  103.0 18.5 %reduce-scatter.10.cloned.1.call-done = f32[32,16,2,16]{1,0,3,2:T(8,128)} async-done(((f32[64,16,2,16]{1,0,3,2:T(8,128)}), f32[32,16,2,16]{1,0,3,2:T(8,128)}) %reduce-scatter.10.cloned.1.call-update) | async-done | bytes 65552 | tf_op jit(solution)/shard_map/reduce_scatter | solution.py:154
  121.6 1.1 broadcast_multiply_fusion.2
  122.7 38.4 %all_gather.15 = f32[32,16,2,64]{1,0,3,2:T(8,128)S(1)} all-gather(f32[32,16,2,16]{1,0,3,2:T(8,128)S(1)} %broadcast_multiply_fusion.2), channel_id=1, replica_groups=mesh['member'=2,'slab'=4,'chan'=2,'mode'=2] {'slab'}, dimensions={3}, use_global_device_ids=true | all-gather | bytes 327680 | tf_op jit(solution)/shard_map/all_gather | solution.py:137
  161.2 1.3 copy.47
  162.5 1.1 fusion.50
  163.6 1.1 fusion.51
  164.8 1.1 fusion.24
  165.9 1.1 fusion.25
  167.1 0.8 copy.48
  167.9 1.7 reshape.289
  169.7 11.1 %all-gather.3.cloned.1.call-done = f32[32,64,256]{2,1,0:T(8,128)} async-done(((f32[32,32,256]{2,1,0:T(8,128)}), f32[32,64,256]{2,1,0:T(8,128)}) %all-gather.3.cloned.1.call-update) | async-done | bytes 2097168 | tf_op jit(solution)/shard_map/all_gather | solution.py:142
  180.9 36.1 %fusion.150 = (f32[32]{0:T(128)}, f32[32]{0:T(128)}, f32[32,256,512]{2,1,0:T(8,128)S(1)}, f32[32,256,512]{2,1,0:T(8,128)}) fusion(f32[32,256,512]{2,1,0:T(8,128)} %param.7, f32[32,256,512]{2,1,0:T(8,128)} %param.8, f32[32]{0:T(128)S(1)} %copy-done.9, f32[32]{0:T(128)S(1)} %copy-done.7, f32[32,64,256]{2,1,0:T(8,128)} %all-gather.3.cloned.1.call-done, ...), kind=kOutput, calls=%fused_computation.205 | convolution fusion | flops 3330277376 | bytes 69337600 | tf_op jit(solution)/shard_map/ckh,wk->chw/dot_general | solution.py:143
  216.9 6.2 %copy-done.4 = f32[32,256,512]{2,1,0:T(8,128)} copy-done((f32[32,256,512]{2,1,0:T(8,128)}, f32[32,256,512]{2,1,0:T(8,128)S(1)}, u32[]{:S(2)}) %copy-start.4) | copy-done | bytes 16777240
  223.1 17.8 %convolution_bitcast_fusion = f32[32,64,256]{2,1,0:T(8,128)} fusion(f32[512,64,1]{0,1,2:T(8,128)S(1)} %reshape.294, f32[32,256,512]{2,1,0:T(8,128)S(1)} %get-tuple-element.9), kind=kOutput, calls=%fused_computation.34 | convolution fusion | flops 3221225472 | bytes 19005440 | tf_op jit(solution)/shard_map/chw,wk->ckh/dot_general | solution.py:128
  241.0 10.9 %reduce-scatter.12.cloned.1.call-done = f32[32,32,256]{2,1,0:T(8,128)} async-done(((f32[32,64,256]{2,1,0:T(8,128)}), f32[32,32,256]{2,1,0:T(8,128)}) %reduce-scatter.12.cloned.1.call-update) | async-done | bytes 1048592 | tf_op jit(solution)/shard_map/reduce_scatter | solution.py:129
  251.9 1.8 reshape.290
  253.7 0.8 fusion.152
  254.5 1.2 fusion.34
  255.7 1.2 fusion.30
  256.9 1.2 fusion.27
  258.1 1.2 fusion.26
  259.3 0.7 pad_maximum_fusion.4
  260.1 21.4 %reduce-scatter.14.cloned.1.call-done = f32[512,2,16]{0,2,1:T(8,128)} async-done(((f32[512,2,64]{0,2,1:T(8,128)}), f32[512,2,16]{0,2,1:T(8,128)}) %reduce-scatter.14.cloned.1.call-update) | async-done | bytes 65552 | tf_op jit(solution)/shard_map/reduce_scatter | solution.py:131
  281.5 1.0 reshape.291
  282.6 11.9 %all_gather.17 = f32[64,16,2,16]{1,0,3,2:T(8,128)S(1)} all-gather(f32[32,16,2,16]{1,0,3,2:T(8,128)S(1)} %broadcast_multiply_fusion.1), channel_id=1, replica_groups=mesh['member'=2,'slab'=4,'chan'=2,'mode'=2] {'chan'}, dimensions={0}, use_global_device_ids=true | all-gather | bytes 196608 | tf_op jit(solution)/shard_map/all_gather | solution.py:163
  294.5 0.3 slice_bitcast_fusion.5
  295.0 11.1 %fusion.16 = f32[16,16,1,32]{3,2,1,0:T(1,128)S(1)} fusion(f32[64,16,16,1]{0,3,2,1:T(1,128)S(1)} %copy.64, f32[32,64,16,16]{1,3,2,0:T(8,128)} %get-tuple-element.11), kind=kOutput, calls=%fused_computation.28 | convolution fusion | flops 6291456 | bytes 2195456 | tf_op jit(solution)/shard_map/oyx,ioyx->iyx/dot_general | solution.py:72
  306.0 10.9 %fusion.6 = f32[16,16,1,32]{3,2,1,0:T(1,128)S(1)} fusion(f32[64,16,16,1]{0,3,2,1:T(1,128)S(1)} %copy.64, f32[32,64,16,16]{1,3,2,0:T(8,128)} %get-tuple-element.12), kind=kOutput, calls=%fused_computation.18 | convolution fusion | flops 6291456 | bytes 2195456 | tf_op jit(solution)/shard_map/oyx,ioyx->iyx/dot_general | solution.py:75
  317.1 11.1 %fusion.14 = f32[16,16,1,32]{3,2,1,0:T(1,128)S(1)} fusion(f32[64,16,16,1]{0,3,2,1:T(1,128)S(1)} %copy.66, f32[32,64,16,16]{1,3,2,0:T(8,128)} %get-tuple-element.11), kind=kOutput, calls=%fused_computation.26 | convolution fusion | flops 6291456 | bytes 2195456 | tf_op jit(solution)/shard_map/oyx,ioyx->iyx/dot_general | solution.py:75
  328.2 10.9 %fusion.8 = f32[16,16,1,32]{3,2,1,0:T(1,128)S(1)} fusion(f32[64,16,16,1]{0,3,2,1:T(1,128)S(1)} %copy.66, f32[32,64,16,16]{1,3,2,0:T(8,128)} %get-tuple-element.12), kind=kOutput, calls=%fused_computation.20 | convolution fusion | flops 6291456 | bytes 2195456 | tf_op jit(solution)/shard_map/oyx,ioyx->iyx/dot_general | solution.py:72
  339.3 19.9 %all_gather.18 = f32[32,16,2,64]{0,1,2,3:T(8,128)S(1)} all-gather(f32[32,16,2,16]{0,1,2,3:T(8,128)S(1)} %pad_maximum_fusion.5), channel_id=1, replica_groups=mesh['member'=2,'slab'=4,'chan'=2,'mode'=2] {'slab'}, dimensions={3}, use_global_device_ids=true | all-gather | bytes 327680 | tf_op jit(solution)/shard_map/all_gather | solution.py:137
  359.3 0.8 copy.49
  360.1 1.1 fusion.52
  361.2 1.1 fusion.53
  362.4 1.1 fusion.22
  363.5 1.1 fusion.23
  364.7 0.8 copy.50
  365.5 1.7 reshape.293
  367.7 14.5 %all-reduce = (f32[32]{0:T(128)}, f32[32]{0:T(128)}) all-reduce(f32[32]{0:T(128)} %get-tuple-element.6, f32[32]{0:T(128)S(1)} %copy-done.10), channel_id=1, replica_groups=mesh['member'=2,'slab'=4,'chan'=2,'mode'=2] {'slab','mode'}, use_global_device_ids=true, to_apply=%region_6.7 | all-reduce | flops 64 | bytes 512 | tf_op jit(solution)/shard_map/psum | solution.py:166
  382.6 2.3 add_bitcast_fusion
  385.0 4.5 %maximum_multiply_fusion = f32[32,64,16,2,16]{1,4,3,2,0:T(8,128)} fusion(f32[32,64,16,1,16]{1,4,3,2,0:T(8,128)S(1)} %get-tuple-element.22, f32[32,64,16,1,16]{1,4,3,2,0:T(8,128)S(1)} %get-tuple-element.21, f32[32,64]{1,0:T(8,128)S(1)} %copy-done.6), kind=kLoop, calls=%fused_computation.12 | loop fusion | flops 2097152 | bytes 8396800 | tf_op jit(solution)/shard_map/mul | solution.py:164
  389.5 21.3 %multiply_add_fusion = f32[32,256,512]{2,1,0:T(8,128)} fusion(f32[32,256,512]{2,1,0:T(8,128)} %copy-done.4, f32[32,64,256]{2,1,0:T(8,128)} %all-gather.5.cloned.1.call-done, f32[512,64,1]{0,1,2:T(8,128)S(1)} %reshape.294, f32[32]{0:T(128)S(1)} %copy-done.7), kind=kOutput, calls=%fused_computation.9 | convolution fusion | flops 3229614080 | bytes 35782784 | tf_op jit(solution)/shard_map/ckh,wk->chw/dot_general | solution.py:143
  (66 shorter events, 3.1 us)
Async XLA Ops:
  7.2 21.7 %copy-start = (s32[64,2]{0,1:T(2,128)S(1)}, s32[64,2]{0,1:T(2,128)}, u32[]{:S(2)}) copy-start(s32[64,2]{0,1:T(2,128)} %param.12) | copy-start | bytes 1540
  7.2 33.9 %reduce-scatter.6.cloned.1.call-start = ((), (), s32[]{:S(2)}) async-start(), calls=%async_computation.5 | async-start | bytes 3145728 | tf_op jit(solution)/shard_map/reduce_scatter | solution.py:129
  7.8 21.3 %copy-start.8 = (s32[64]{0:T(128)S(1)}, s32[64]{0:T(128)}, u32[]{:S(2)}) copy-start(s32[64]{0:T(128)} %param.13) | copy-start | bytes 772
  28.5 42.1 %reduce-scatter.8.cloned.1.call-start = ((), (), s32[]{:S(2)}) async-start(), calls=%async_computation.6 | async-start | bytes 327680 | tf_op jit(solution)/shard_map/reduce_scatter | solution.py:131
  29.2 0.6 copy-start.5
  49.2 72.4 %reduce-scatter.10.cloned.1.call-start = ((), (), s32[]{:S(2)}) async-start(), calls=%async_computation.7 | async-start | bytes 1572864 | tf_op jit(solution)/shard_map/reduce_scatter | solution.py:154
  72.1 17.0 %copy-start.3 = (f32[32,64,16,16]{1,3,2,0:T(8,128)S(1)}, f32[32,64,16,16]{1,3,2,0:T(8,128)}, u32[]{:S(2)}) copy-start(f32[32,64,16,16]{1,3,2,0:T(8,128)} %get-tuple-element.11) | copy-start | bytes 6291460
  72.1 23.1 %copy-start.2 = (f32[32,64,16,16]{1,3,2,0:T(8,128)S(1)}, f32[32,64,16,16]{1,3,2,0:T(8,128)}, u32[]{:S(2)}) copy-start(f32[32,64,16,16]{1,3,2,0:T(8,128)} %get-tuple-element.12) | copy-start | bytes 6291460
  102.8 78.0 %all-gather.3.cloned.1.call-start = ((), (), s32[]{:S(2)}) async-start(), calls=%async_computation.8 | async-start | bytes 3145728 | tf_op jit(solution)/shard_map/all_gather | solution.py:142
  122.7 58.1 %copy-start.7 = (f32[32]{0:T(128)S(1)}, f32[32]{0:T(128)}, u32[]{:S(2)}) copy-start(f32[32]{0:T(128)} %param.10) | copy-start | bytes 388
  122.7 58.1 %copy-start.9 = (f32[32]{0:T(128)S(1)}, f32[32]{0:T(128)}, u32[]{:S(2)}) copy-start(f32[32]{0:T(128)} %param.11) | copy-start | bytes 388
  169.7 82.2 %reduce-scatter.12.cloned.1.call-start = ((), (), s32[]{:S(2)}) async-start(), calls=%async_computation.9 | async-start | bytes 3145728 | tf_op jit(solution)/shard_map/reduce_scatter | solution.py:129
  216.9 6.2 %copy-start.4 = (f32[32,256,512]{2,1,0:T(8,128)}, f32[32,256,512]{2,1,0:T(8,128)S(1)}, u32[]{:S(2)}) copy-start(f32[32,256,512]{2,1,0:T(8,128)S(1)} %get-tuple-element.9) | copy-start | bytes 50331652
  240.9 40.6 %reduce-scatter.14.cloned.1.call-start = ((), (), s32[]{:S(2)}) async-start(), calls=%async_computation.10 | async-start | bytes 327680 | tf_op jit(solution)/shard_map/reduce_scatter | solution.py:131
  260.0 129.5 %all-gather.5.cloned.1.call-start = ((), (), s32[]{:S(2)}) async-start(), calls=%async_computation.11 | async-start | bytes 3145728 | tf_op jit(solution)/shard_map/all_gather | solution.py:142
  339.1 28.6 %copy-start.10 = (f32[32]{0:T(128)S(1)}, f32[32]{0:T(128)}, u32[]{:S(2)}) copy-start(f32[32]{0:T(128)} %get-tuple-element.5) | copy-start | bytes 388
  364.7 20.2 %copy-start.6 = (f32[32,64]{1,0:T(8,128)S(1)}, f32[32,64]{1,0:T(8,128)}, u32[]{:S(2)}) copy-start(f32[32,64]{1,0:T(8,128)} %copy-done.5) | copy-start | bytes 24580
  389.5 21.3 %copy-start.1 = (s32[64,2]{0,1:T(2,128)S(1)}, s32[64,2]{0,1:T(2,128)}, u32[]{:S(2)}) copy-start(s32[64,2]{0,1:T(2,128)} %param.12) | copy-start | bytes 1540
Sparse Core Ops, SparseCore 0:
  28.6 12.3 reduce-scatter.5
  49.3 21.2 reduce-scatter.7
  103.0 18.5 reduce-scatter.9
  169.8 11.0 all-gather.2
  241.0 10.7 reduce-scatter.11
  260.1 21.2 reduce-scatter.13
  367.4 10.3 all-gather.4
where the time goes:
time: 424 us; the launch traced here: 418 us
  matrix products  188 us (44%)
  blocking collectives  84.8 us (20%)
  waiting for transfers between devices  78.2 us (18%)
  local copies, waits for them, and re-layouts  32.6 us (8%)
  other arithmetic  19.1 us (5%)
  between operations  15.1 us (4%)
    all_gather x2, blocking collectives, synthesis(): whole_modes = lax.all_gather(modes_in, 'slab', axis=3, tiled=True)  58.4 us
    dot_general x2, matrix products, synthesis(): return jnp.einsum('ckh,wk->chw', gathered, column_tab, precision=precise)  57.4 us
    dot_general x2, matrix products, spectrum(): jnp.einsum('chw,wk->ckh', values, column_tab, precision=precise)  38.5 us
    reduce_scatter x2, waiting for transfers between devices, spectrum(): lax.psum_scatter(row_forward(paired, row_cos, row_sin), 'slab', scatter_d...  34.8 us
    reduce_scatter x1, waiting for transfers between devices, local(): lax.psum_scatter(contract(spectra, masked_weight), 'chan', scatter_dimens...  18.5 us
    psum x1, blocking collectives, local(): lax.psum((jnp.sum(grad_sum * source_field, axis=(1, 2)), jnp.sum(grad_sum...  14.5 us
    reduce_scatter x2, waiting for transfers between devices, spectrum(): lax.psum_scatter(partial_cols, 'mode', scatter_dimension=1, tiled=True)  13.6 us
    all_gather x1, blocking collectives, local(): all_grads = lax.all_gather(grad_modes, 'chan', axis=0, tiled=True)  11.9 us
  transfers between devices with their start and end apart: 7, of which 6 were waited for; matrix products, arithmetic and copies ran while one was open for 6% of the time, Pallas kernels for 0%

commit v1 on v0

--- a/solution.py
+++ b/solution.py
@@ -5,6 +5,12 @@
 from jax.sharding import PartitionSpec as P
 
 precise = lax.Precision.HIGHEST
+
+
+def divide_islands(v0):
+    x_now = jax.lax.all_gather(v0, "slab")
+    then = jnp.concatenate(x_now, 3)
+    return then
 
 
 def column_table(extent, freq_count, first_cell, cell_count):
@@ -134,7 +140,7 @@
         return spectra.reshape(values.shape[0], local_freq, 2, local_kx)
 
     def synthesis(modes_in):
-        whole_modes = lax.all_gather(modes_in, "slab", axis=3, tiled=True)
+        whole_modes = divide_islands(modes_in)
         rebuilt = row_inverse(
             whole_modes.reshape(channels * local_freq, 2, kx_count), row_cos, row_sin
         )

time: 424 us -> 409 us (0.965)
  matrix products: 188 us -> 144 us
  blocking collectives: 84.8 us -> 99.6 us
  other arithmetic: 19.1 us -> 30.9 us
    dot_general x4 -> x0, matrix products: 43.9 us -> none  [the longest x1 11.1 us: contract_back(): jnp.einsum('oyx,ioyx->iyx', grad_imag, weight_real, precision=precise)]
    all_gather x2, blocking collectives: 58.4 us -> 73.3 us  [divide_islands(): x_now = jax.lax.all_gather(v0, 'slab')]
    another operation x1, other arithmetic: 2.33 us -> 10.6 us  [outer_grad(): return jnp.stack([real_side, imag_side], axis=3)]
where the time goes in v1:
time: 409 us; the launch traced here: 404 us
  matrix products  144 us (35%)
  blocking collectives  99.6 us (24%)
  waiting for transfers between devices  78.4 us (19%)
  local copies, waits for them, and re-layouts  35.6 us (9%)
  other arithmetic  30.9 us (8%)
  between operations  14.8 us (4%)
    all_gather x2, blocking collectives, divide_islands(): x_now = jax.lax.all_gather(v0, 'slab')  73.3 us
    dot_general x2, matrix products, synthesis(): return jnp.einsum('ckh,wk->chw', gathered, column_tab, precision=precise)  57.5 us
    dot_general x2, matrix products, spectrum(): jnp.einsum('chw,wk->ckh', values, column_tab, precision=precise)  38.3 us
    reduce_scatter x2, waiting for transfers between devices, spectrum(): lax.psum_scatter(row_forward(paired, row_cos, row_sin), 'slab', scatter_d...  34.3 us
    reduce_scatter x1, waiting for transfers between devices, local(): lax.psum_scatter(contract(spectra, masked_weight), 'chan', scatter_dimens...  18.5 us
    psum x1, blocking collectives, local(): lax.psum((jnp.sum(grad_sum * source_field, axis=(1, 2)), jnp.sum(grad_sum...  14.4 us
    reduce_scatter x2, waiting for transfers between devices, spectrum(): lax.psum_scatter(partial_cols, 'mode', scatter_dimension=1, tiled=True)  14.3 us
    all_gather x1, blocking collectives, local(): all_grads = lax.all_gather(grad_modes, 'chan', axis=0, tiled=True)  11.9 us
  transfers between devices with their start and end apart: 7, of which 6 were waited for; matrix products, arithmetic and copies ran while one was open for 6% of the time, Pallas kernels for 0%

profile of v1, /device:TPU:0, one launch (start us, length us, event | category | flops | bytes accessed | tf_op | source)
XLA Modules:
  0.0 403.7 jit_solution(15987355409895090514)
XLA Ops:
  7.2 0.3 fusion.77
  7.8 20.7 %convolution_bitcast_fusion.1 = f32[32,64,256]{2,1,0:T(8,128)} fusion(f32[512,64,1]{0,1,2:T(8,128)S(1)} %reshape.296, f32[32,256,512]{2,1,0:T(8,128)} %param.7), kind=kOutput, calls=%fused_computation.36 | convolution fusion | flops 3221225472 | bytes 19005440 | tf_op jit(solution)/shard_map/chw,wk->ckh/dot_general | solution.py:134
  28.5 0.2 reduce-scatter.8.cloned.1.call-start
  29.1 8.5 %broadcast_multiply_fusion = f32[32,64,16,2,16]{1,4,3,2,0:T(8,128)} fusion(f32[32,64,16,2,16]{1,4,3,2,0:T(8,128)} %param.9, f32[32,64]{1,0:T(8,128)S(1)} %compare_convert_fusion), kind=kLoop, calls=%fused_computation.23 | loop fusion | flops 1048576 | bytes 8396800 | tf_op jit(solution)/shard_map/mul | solution.py:157
  37.6 3.4 reduce-scatter.6.cloned.1.call-done
  41.0 1.8 reshape.286
  42.9 0.8 fusion.147
  43.7 1.2 fusion.36
  44.9 1.2 fusion.32
  46.1 1.2 fusion.25
  47.3 1.2 fusion.24
  48.5 0.7 pad_maximum_fusion.3
  49.2 0.3 reduce-scatter.10.cloned.1.call-start
  49.5 7.9 %slice_bitcast_fusion.1 = (f32[32,64,16,16]{1,3,2,0:T(8,128)}, f32[32,64,16,16]{1,3,2,0:T(8,128)}) fusion(f32[32,64,16,2,16]{1,4,3,2,0:T(8,128)} %broadcast_multiply_fusion), kind=kLoop, calls=%fused_computation.33 | loop fusion | bytes 8388608 | tf_op jit(solution)/shard_map/squeeze | solution.py:62
  57.4 13.3 %reduce-scatter.8.cloned.1.call-done = f32[512,2,16]{0,2,1:T(8,128)} async-done(((f32[512,2,64]{0,2,1:T(8,128)}), f32[512,2,16]{0,2,1:T(8,128)}) %reduce-scatter.8.cloned.1.call-update) | async-done | bytes 65552 | tf_op jit(solution)/shard_map/reduce_scatter | solution.py:137
  70.7 1.0 reshape.287
  71.7 0.8 slice_bitcast_fusion.7
  72.8 8.3 %fusion.14 = f32[16,16,1,64]{3,2,1,0:T(1,128)S(1)} fusion(f32[32,16,16,1]{0,3,2,1:T(1,128)S(1)} %copy.72, f32[32,64,16,16]{1,3,2,0:T(8,128)} %get-tuple-element.17), kind=kOutput, calls=%fused_computation.28 | convolution fusion | flops 6291456 | bytes 2195456 | tf_op jit(solution)/shard_map/iyx,ioyx->oyx/dot_general | solution.py:67
  81.2 8.6 %fusion.16 = f32[16,16,1,64]{3,2,1,0:T(1,128)S(1)} fusion(f32[32,16,16,1]{0,3,2,1:T(1,128)S(1)} %copy.69, f32[32,64,16,16]{1,3,2,0:T(8,128)} %get-tuple-element.17), kind=kOutput, calls=%fused_computation.30 | convolution fusion | flops 6291456 | bytes 2195456 | tf_op jit(solution)/shard_map/iyx,ioyx->oyx/dot_general | solution.py:64
  89.8 6.0 %fusion.10 = f32[16,16,1,64]{3,2,1,0:T(1,128)S(1)} fusion(f32[32,16,16,1]{0,3,2,1:T(1,128)S(1)} %copy.69, f32[32,64,16,16]{1,3,2,0:T(8,128)S(1)} %copy-done.3), kind=kOutput, calls=%fused_computation.24 | convolution fusion | flops 6291456 | bytes 2195456 | tf_op jit(solution)/shard_map/iyx,ioyx->oyx/dot_general | solution.py:67
  95.9 6.2 %fusion.12 = f32[16,16,1,64]{3,2,1,0:T(1,128)S(1)} fusion(f32[32,16,16,1]{0,3,2,1:T(1,128)S(1)} %copy.72, f32[32,64,16,16]{1,3,2,0:T(8,128)S(1)} %copy-done.3), kind=kOutput, calls=%fused_computation.26 | convolution fusion | flops 6291456 | bytes 2195456 | tf_op jit(solution)/shard_map/iyx,ioyx->oyx/dot_general | solution.py:64
  102.2 1.3 copy.57
  103.7 18.5 %reduce-scatter.10.cloned.1.call-done = f32[32,16,2,16]{1,0,3,2:T(8,128)} async-done(((f32[64,16,2,16]{1,0,3,2:T(8,128)}), f32[32,16,2,16]{1,0,3,2:T(8,128)}) %reduce-scatter.10.cloned.1.call-update) | async-done | bytes 65552 | tf_op jit(solution)/shard_map/reduce_scatter | solution.py:160
  122.3 1.1 broadcast_multiply_fusion.2
  123.4 38.3 %all-gather = f32[128,16,2,16]{1,0,3,2:T(8,128)S(1)} all-gather(f32[32,16,2,16]{1,0,3,2:T(8,128)S(1)} %broadcast_multiply_fusion.2), channel_id=2, replica_groups=mesh['member'=2,'slab'=4,'chan'=2,'mode'=2] {'slab'}, dimensions={0}, use_global_device_ids=true | all-gather | bytes 327680 | tf_op jit(solution)/shard_map/all_gather | solution.py:11
  161.8 0.2 copy.150
  162.0 1.6 reshape_reshape.6
  163.5 1.1 fusion.49
  164.7 1.1 fusion.50
  165.8 1.1 fusion.20
  167.0 1.1 fusion.21
  168.2 0.8 copy.59
  169.0 1.7 reshape.289
  170.8 11.1 %all-gather.5.cloned.1.call-done = f32[32,64,256]{2,1,0:T(8,128)} async-done(((f32[32,32,256]{2,1,0:T(8,128)}), f32[32,64,256]{2,1,0:T(8,128)}) %all-gather.5.cloned.1.call-update) | async-done | bytes 2097168 | tf_op jit(solution)/shard_map/all_gather | solution.py:148
  181.9 36.3 %fusion.144 = (f32[32]{0:T(128)}, f32[32]{0:T(128)}, f32[32,256,512]{2,1,0:T(8,128)S(1)}, f32[32,256,512]{2,1,0:T(8,128)}) fusion(f32[32,256,512]{2,1,0:T(8,128)} %param.7, f32[32,256,512]{2,1,0:T(8,128)} %param.8, f32[32]{0:T(128)S(1)} %copy-done.9, f32[32]{0:T(128)S(1)} %copy-done.7, f32[32,64,256]{2,1,0:T(8,128)} %all-gather.5.cloned.1.call-done, ...), kind=kOutput, calls=%fused_computation.202 | convolution fusion | flops 3330277376 | bytes 69337600 | tf_op jit(solution)/shard_map/ckh,wk->chw/dot_general | solution.py:149
  218.2 6.2 %copy-done.2 = f32[32,256,512]{2,1,0:T(8,128)} copy-done((f32[32,256,512]{2,1,0:T(8,128)}, f32[32,256,512]{2,1,0:T(8,128)S(1)}, u32[]{:S(2)}) %copy-start.2) | copy-done | bytes 16777240
  224.4 17.6 %convolution_bitcast_fusion = f32[32,64,256]{2,1,0:T(8,128)} fusion(f32[512,64,1]{0,1,2:T(8,128)S(1)} %reshape.296, f32[32,256,512]{2,1,0:T(8,128)S(1)} %get-tuple-element.15), kind=kOutput, calls=%fused_computation.35 | convolution fusion | flops 3221225472 | bytes 19005440 | tf_op jit(solution)/shard_map/chw,wk->ckh/dot_general | solution.py:134
  242.0 10.9 %reduce-scatter.12.cloned.1.call-done = f32[32,32,256]{2,1,0:T(8,128)} async-done(((f32[32,64,256]{2,1,0:T(8,128)}), f32[32,32,256]{2,1,0:T(8,128)}) %reduce-scatter.12.cloned.1.call-update) | async-done | bytes 1048592 | tf_op jit(solution)/shard_map/reduce_scatter | solution.py:135
  252.9 1.8 reshape.290
  254.8 0.8 fusion.146
  255.6 1.2 fusion.30
  256.8 1.2 fusion.26
  257.9 1.2 fusion.23
  259.1 1.2 fusion.22
  260.3 0.7 pad_maximum_fusion.5
  261.1 0.2 copy.64
  261.3 0.2 copy.66
  261.5 21.0 %reduce-scatter.14.cloned.1.call-done = f32[512,2,16]{0,2,1:T(8,128)} async-done(((f32[512,2,64]{0,2,1:T(8,128)}), f32[512,2,16]{0,2,1:T(8,128)}) %reduce-scatter.14.cloned.1.call-update) | async-done | bytes 65552 | tf_op jit(solution)/shard_map/reduce_scatter | solution.py:137
  282.5 1.0 reshape.291
  283.6 11.9 %all_gather.24 = f32[64,16,2,16]{1,0,3,2:T(8,128)S(1)} all-gather(f32[32,16,2,16]{1,0,3,2:T(8,128)S(1)} %broadcast_multiply_fusion.1), channel_id=1, replica_groups=mesh['member'=2,'slab'=4,'chan'=2,'mode'=2] {'chan'}, dimensions={0}, use_global_device_ids=true | all-gather | bytes 196608 | tf_op jit(solution)/shard_map/all_gather | solution.py:169
  296.0 10.6 %add_bitcast_fusion = (f32[32,64,16,1,16]{1,4,3,2,0:T(8,128)}, f32[32,64,16,1,16]{1,4,3,2,0:T(8,128)}, f32[16,16,32]{1,0,2:T(8,128)S(1)}, f32[16,16,32]{1,0,2:T(...) fusion(f32[16,16,64]{2,1,0:T(8,128)S(1)} %copy.106, f32[16,16,64]{2,1,0:T(8,128)S(1)} %copy.105, ...), kind=kLoop, calls=%fused_computation.22 | loop fusion | flops 7307264 | bytes 8716288 | tf_op jit(solution)/shard_map/stack | solution.py:98
  306.7 35.0 %all-gather.1 = f32[128,16,2,16]{3,1,2,0:T(8,128)S(1)} all-gather(f32[32,16,2,16]{3,1,2,0:T(8,128)S(1)} %pad_maximum_fusion.2), channel_id=3, replica_groups=mesh['member'=2,'slab'=4,'chan'=2,'mode'=2] {'slab'}, dimensions={0}, use_global_device_ids=true | all-gather | bytes 327680 | tf_op jit(solution)/shard_map/all_gather | solution.py:11
  341.7 1.3 copy.100
  343.1 0.8 copy.61
  343.9 1.6 reshape_reshape.7
  345.5 1.1 fusion.51
  346.7 1.1 fusion.52
  347.8 1.1 fusion.18
  348.9 1.1 fusion.19
  350.2 0.8 copy.62
  351.0 1.7 reshape.293
  352.7 14.4 %all-reduce = (f32[32]{0:T(128)}, f32[32]{0:T(128)}) all-reduce(f32[32]{0:T(128)S(1)} %copy-done.11, f32[32]{0:T(128)S(1)} %copy-done.10), channel_id=1, replica_groups=mesh['member'=2,'slab'=4,'chan'=2,'mode'=2] {'slab','mode'}, use_global_device_ids=true, to_apply=%region_6.7 | all-reduce | flops 64 | bytes 512 | tf_op jit(solution)/shard_map/psum | solution.py:172
  367.1 8.2 %maximum_multiply_fusion = f32[32,64,16,2,16]{1,4,3,2,0:T(8,128)} fusion(f32[32,64,16,1,16]{1,4,3,2,0:T(8,128)} %get-tuple-element.26, f32[32,64,16,1,16]{1,4,3,2,0:T(8,128)} %get-tuple-element.25, f32[32,64]{1,0:T(8,128)S(1)} %copy-done.6), kind=kLoop, calls=%fused_computation.12 | loop fusion | flops 2097152 | bytes 8396800 | tf_op jit(solution)/shard_map/mul | solution.py:170
  375.3 21.3 %multiply_add_fusion = f32[32,256,512]{2,1,0:T(8,128)} fusion(f32[32,256,512]{2,1,0:T(8,128)} %copy-done.2, f32[32,64,256]{2,1,0:T(8,128)} %all-gather.7.cloned.1.call-done, f32[512,64,1]{0,1,2:T(8,128)S(1)} %reshape.296, f32[32]{0:T(128)S(1)} %copy-done.7), kind=kOutput, calls=%fused_computation.9 | convolution fusion | flops 3229614080 | bytes 35782784 | tf_op jit(solution)/shard_map/ckh,wk->chw/dot_general | solution.py:149
  (65 shorter events, 2.2 us)
Async XLA Ops:
  7.2 21.6 %copy-start = (s32[64,2]{0,1:T(2,128)S(1)}, s32[64,2]{0,1:T(2,128)}, u32[]{:S(2)}) copy-start(s32[64,2]{0,1:T(2,128)} %param.12) | copy-start | bytes 1540
  7.2 33.9 %reduce-scatter.6.cloned.1.call-start = ((), (), s32[]{:S(2)}) async-start(), calls=%async_computation.5 | async-start | bytes 3145728 | tf_op jit(solution)/shard_map/reduce_scatter | solution.py:135
  7.8 21.3 %copy-start.8 = (s32[64]{0:T(128)S(1)}, s32[64]{0:T(128)}, u32[]{:S(2)}) copy-start(s32[64]{0:T(128)} %param.13) | copy-start | bytes 772
  28.5 42.1 %reduce-scatter.8.cloned.1.call-start = ((), (), s32[]{:S(2)}) async-start(), calls=%async_computation.6 | async-start | bytes 327680 | tf_op jit(solution)/shard_map/reduce_scatter | solution.py:137
  29.1 8.5 %copy-start.5 = (f32[32,64]{1,0:T(8,128)}, f32[32,64]{1,0:T(8,128)S(1)}, u32[]{:S(2)}) copy-start(f32[32,64]{1,0:T(8,128)S(1)} %compare_convert_fusion) | copy-start | bytes 24580
  49.2 73.1 %reduce-scatter.10.cloned.1.call-start = ((), (), s32[]{:S(2)}) async-start(), calls=%async_computation.7 | async-start | bytes 1572864 | tf_op jit(solution)/shard_map/reduce_scatter | solution.py:160
  72.8 17.0 %copy-start.3 = (f32[32,64,16,16]{1,3,2,0:T(8,128)S(1)}, f32[32,64,16,16]{1,3,2,0:T(8,128)}, u32[]{:S(2)}) copy-start(f32[32,64,16,16]{1,3,2,0:T(8,128)} %get-tuple-element.18) | copy-start | bytes 6291460
  103.5 78.4 %all-gather.5.cloned.1.call-start = ((), (), s32[]{:S(2)}) async-start(), calls=%async_computation.8 | async-start | bytes 3145728 | tf_op jit(solution)/shard_map/all_gather | solution.py:148
  161.8 20.2 %copy-start.7 = (f32[32]{0:T(128)S(1)}, f32[32]{0:T(128)}, u32[]{:S(2)}) copy-start(f32[32]{0:T(128)} %param.10) | copy-start | bytes 388
  161.8 20.2 %copy-start.9 = (f32[32]{0:T(128)S(1)}, f32[32]{0:T(128)}, u32[]{:S(2)}) copy-start(f32[32]{0:T(128)} %param.11) | copy-start | bytes 388
  170.7 82.2 %reduce-scatter.12.cloned.1.call-start = ((), (), s32[]{:S(2)}) async-start(), calls=%async_computation.9 | async-start | bytes 3145728 | tf_op jit(solution)/shard_map/reduce_scatter | solution.py:135
  218.2 6.2 %copy-start.2 = (f32[32,256,512]{2,1,0:T(8,128)}, f32[32,256,512]{2,1,0:T(8,128)S(1)}, u32[]{:S(2)}) copy-start(f32[32,256,512]{2,1,0:T(8,128)S(1)} %get-tuple-element.15) | copy-start | bytes 50331652
  241.9 19.2 %copy-start.4 = (f32[16,16,32]{0,2,1:T(8,128)S(1)}, f32[16,16,32]{0,2,1:T(8,128)}, u32[]{:S(2)}) copy-start(f32[16,16,32]{0,2,1:T(8,128)} %get-tuple-element.27) | copy-start | bytes 98308
  242.0 40.6 %reduce-scatter.14.cloned.1.call-start = ((), (), s32[]{:S(2)}) async-start(), calls=%async_computation.10 | async-start | bytes 327680 | tf_op jit(solution)/shard_map/reduce_scatter | solution.py:137
  261.1 114.2 %all-gather.7.cloned.1.call-start = ((), (), s32[]{:S(2)}) async-start(), calls=%async_computation.11 | async-start | bytes 3145728 | tf_op jit(solution)/shard_map/all_gather | solution.py:148
  343.1 9.7 %copy-start.10 = (f32[32]{0:T(128)S(1)}, f32[32]{0:T(128)}, u32[]{:S(2)}) copy-start(f32[32]{0:T(128)} %get-tuple-element.5) | copy-start | bytes 388
  343.1 9.7 %copy-start.11 = (f32[32]{0:T(128)S(1)}, f32[32]{0:T(128)}, u32[]{:S(2)}) copy-start(f32[32]{0:T(128)} %get-tuple-element.6) | copy-start | bytes 388
  343.1 24.0 %copy-start.6 = (f32[32,64]{1,0:T(8,128)S(1)}, f32[32,64]{1,0:T(8,128)}, u32[]{:S(2)}) copy-start(f32[32,64]{1,0:T(8,128)} %copy-done.5) | copy-start | bytes 24580
  375.3 21.3 %copy-start.1 = (s32[64,2]{0,1:T(2,128)S(1)}, s32[64,2]{0,1:T(2,128)}, u32[]{:S(2)}) copy-start(s32[64,2]{0,1:T(2,128)} %param.12) | copy-start | bytes 1540
Sparse Core Ops, SparseCore 0:
  28.6 12.3 reduce-scatter.5
  49.3 21.2 reduce-scatter.7
  103.7 18.5 reduce-scatter.9
  170.9 11.0 all-gather.4
  242.1 10.7 reduce-scatter.11
  261.2 21.2 reduce-scatter.13
  352.8 10.4 all-gather.6
